TPU v7x, 16 devices: a 4x2x1 block of a 4x4x8 slice. The times are simulated.
16 devices in a mesh: data: 2 (over y, z), expert: 8 (over x, core).
Axes of the slice: x: 4, y: 2, z: 1, core: 2. Of those that a mesh axis runs over, the one named last changes fastest.
The devices are a block of a 4x4x8 slice.
Arguments:
- x: bfloat16 [4096, 2048], P(('data', 'expert')), parts along dimension 0
- idx: int32 [4096, 6], P(('data', 'expert')), parts along dimension 0
- g: float32 [4096, 6], P(('data', 'expert')), parts along dimension 0
- hot_tok: int32 [2048], P(('data', 'expert')), parts along dimension 0
- W1: bfloat16 [64, 2048, 1408], P('expert')
- W3: bfloat16 [64, 2048, 1408], P('expert')
- W2: bfloat16 [64, 1408, 2048], P('expert')
Outputs:
- output: bfloat16 [4096, 2048], P(('data', 'expert')), parts along dimension 0
There are 2 independent parts. A program takes and returns all parts, laid end to end along the dimension named above; an argument that names none is the same for every part.
All inputs are finite; a program needn't handle non-finite values.
Results may differ from a plain program's by a relative error of at most 0.001.
Values are sent between devices in bfloat16 or wider.
A program may use at most 768 MiB of HBM per device.

v0:
```python
import jax
import jax.numpy as jnp
from jax import lax
from jax.sharding import PartitionSpec as P


def _dest(idx, hot_tok, n, el, ch, cap):
    t, k = idx.shape
    s = ch + (el - 1) * cap
    flat = idx.reshape(-1)
    onehot = (flat[:, None] == jnp.arange(n * el, dtype=jnp.int32)[None, :]).astype(jnp.int32)
    rank = jnp.take_along_axis(jnp.cumsum(onehot, axis=0) - onehot, flat[:, None], axis=1).reshape(t, k)
    hot_rank = jnp.zeros((t,), jnp.int32).at[hot_tok].set(jnp.arange(ch, dtype=jnp.int32))
    loc = idx % el
    pos = (idx // el) * s + jnp.where(loc == 0, rank, ch + (loc - 1) * cap + rank)
    return jnp.where(idx == 0, hot_rank[:, None], pos)


def _send(x, dest, rows):
    t, d = x.shape
    k = dest.shape[1]
    src = jnp.full((rows,), t, jnp.int32).at[dest.reshape(-1)].set(jnp.repeat(jnp.arange(t, dtype=jnp.int32), k))
    return jnp.concatenate([x, jnp.zeros((1, d), x.dtype)])[src]


def _combine(back, dest, g):
    y = jnp.zeros((dest.shape[0], back.shape[1]), jnp.float32)
    for j in range(dest.shape[1]):
        y = y + g[:, j:j + 1] * back[dest[:, j]].astype(jnp.float32)
    return y.astype(jnp.bfloat16)


def _experts(xs, w1, w3, w2, form_in, form_out):
    a = jnp.einsum(form_in, xs, w1, preferred_element_type=jnp.float32)
    b = jnp.einsum(form_in, xs, w3, preferred_element_type=jnp.float32)
    u = (jax.nn.silu(a) * b).astype(jnp.bfloat16)
    return jnp.einsum(form_out, u, w2, preferred_element_type=jnp.float32).astype(jnp.bfloat16)


def solution(mesh):
    n = mesh.shape['expert']

    def local(x, idx, g, hot_tok, w1, w3, w2):
        t, d = x.shape
        k = idx.shape[1]
        el = w1.shape[0]
        e = el * n
        ch = hot_tok.shape[0]
        cap = 2 * ((t * k - ch + e - 2) // (e - 1))
        s = ch + (el - 1) * cap
        dest = _dest(idx, hot_tok, n, el, ch, cap)
        send = _send(x, dest, n * s).reshape(n, s, d)
        recv = lax.all_to_all(send, 'expert', 0, 0, tiled=True)
        out = _experts(recv[:, :ch], w1[0], w3[0], w2[0], 'rcd,df->rcf', 'rcf,fd->rcd')
        if el > 1:
            xc = recv[:, ch:].reshape(n, el - 1, cap, d)
            oc = _experts(xc, w1[1:], w3[1:], w2[1:], 'recd,edf->recf', 'recf,efd->recd')
            out = jnp.concatenate([out, oc.reshape(n, (el - 1) * cap, d)], axis=1)
        back = lax.all_to_all(out, 'expert', 0, 0, tiled=True)
        return _combine(back.reshape(n * s, d), dest, g)

    rows = P(('data', 'expert'))
    wspec = P('expert')
    return jax.shard_map(local, mesh=mesh, in_specs=(rows, rows, rows, rows, wspec, wspec, wspec), out_specs=rows, check_vma=False)
```

profile of v0, /device:TPU:112, one launch (start us, length us, event | category | flops | bytes accessed | tf_op | source)
XLA Modules:
  0.0 679.0 jit_solution(11109911742374587215)
XLA Ops:
  0.0 0.9 copy.68
  0.9 0.1 broadcast_in_dim_reshape.4
  1.1 0.1 eq.39
  1.2 0.1 eq.35
  1.4 0.7 compare_select_fusion.9
  2.1 0.1 reshape.223
  2.3 18.1 %reduce-window.6 = s32[64,12,128]{2,1,0:T(8,128)S(1)} reduce-window(s32[64,12,128]{2,1,0:T(8,128)S(1)} %fusion.39, s32[]{:T(128)} %constant.42.clone.1), window={size=1x1x128 pad=0_0x0_0x127_0}, to_apply=%region_1.2 | reduce-window | flops 12484608 | bytes 786436 | tf_op jit(solution)/shard_map/reduce-window
  20.4 0.2 slice.104
  20.7 0.3 copy.69
  21.0 0.1 copy.70
  21.1 0.2 broadcast_add_fusion
  21.3 0.1 fusion.40
  21.4 12.7 %gather_fusion.7 = s32[1536]{0:T(1024)S(1)} fusion(s32[1536,64]{0,1:T(8,128)S(1)} %fusion.40, s32[1536]{0:T(1024)S(1)} %fusion.52), kind=kCustom, calls=%fused_computation.7 | custom fusion | bytes 24576 | tf_op jit(solution)/shard_map/jit(take_along_axis)/gather | solution.py:12
  34.1 0.1 gather.28
  34.3 0.1 copy.73
  34.4 1.0 scatter_custom_fusion
  35.4 0.0 copy-done.5
  35.4 0.0 copy-start.3
  35.4 0.1 copy.74
  35.5 0.1 reshape.141
  35.7 6.2 scatter_custom_fusion.1
  42.0 0.0 copy-done.2
  42.0 0.1 concatenate.6
  42.1 15.1 %gather_fusion = bf16[3600,2048]{1,0:T(8,128)(2,1)} fusion(bf16[257,2048]{1,0:T(8,128)(2,1)S(1)} %concatenate.6, s32[4096]{0:T(1024)S(1)} %pad_clamp_fusion), kind=kCustom, calls=%fused_computation | custom fusion | bytes 29505600 | tf_op jit(solution)/shard_map/gather | solution.py:23
  57.2 16.0 %reshape.143 = bf16[8,450,2048]{2,1,0:T(8,128)(2,1)} reshape(bf16[3600,2048]{1,0:T(8,128)(2,1)} %gather_fusion) | data formatting | bytes 29491200 | tf_op jit(solution)/shard_map/reshape | solution.py:52
  73.3 170.2 %all_to_all.10 = bf16[8,450,2048]{2,1,0:T(8,128)(2,1)S(1)} all-to-all(bf16[8,450,2048]{2,1,0:T(8,128)(2,1)} %reshape.143), channel_id=1, replica_groups=mesh['data'=2,'expert'=8] {'expert'}, dimensions={0} | all-to-all | bytes 29491200 | tf_op jit(solution)/shard_map/all_to_all | solution.py:53
  243.5 1.4 slice.109
  244.9 17.3 %copy.75 = bf16[8,322,2048]{2,0,1:T(8,128)(2,1)} copy(bf16[8,322,2048]{2,1,0:T(8,128)(2,1)S(1)} %slice.109) | data formatting | bytes 21102592 | tf_op jit(solution)/shard_map/slice | solution.py:56
  262.2 10.6 %fusion.21 = f32[8,128,1408]{2,1,0:T(8,128)} fusion(bf16[8,2048,1408]{2,1,0:T(8,128)(2,1)} %param.12, bf16[8,450,2048]{2,1,0:T(8,128)(2,1)S(1)} %all_to_all.10), kind=kOutput, calls=%fused_computation.32 | convolution fusion | flops 5905580032 | bytes 15728640 | tf_op jit(solution)/shard_map/rcd,df->rcf/dot_general | solution.py:35
  272.7 22.7 %fusion.30 = bf16[8,128,2048]{2,1,0:T(8,128)(2,1)} fusion(bf16[8,1408,2048]{2,1,0:T(8,128)(2,1)} %param.13, f32[8,128,1408]{2,1,0:T(8,128)} %fusion.21, bf16[8,2048,1408]{2,1,0:T(8,128)(2,1)} %param.11, bf16[8,450,2048]{2,1,0:T(8,128)(2,1)} %copy-done), kind=kOutput, calls=%fused_computation.40 | convolution fusion | flops 11821907968 | bytes 25690112 | tf_op jit(solution)/shard_map/rcf,fd->rcd/dot_general | solution.py:37
  295.4 6.5 copy.79
  301.9 30.2 %fusion.2 = f32[7,8,46,1408]{3,2,1,0:T(8,128)} fusion(bf16[8,2048,1408]{2,1,0:T(8,128)(2,1)} %param.12, bf16[8,7,46,2048]{3,0,2,1:T(8,128)(2,1)} %bitcast.87), kind=kOutput, calls=%fused_computation.12 | convolution fusion | flops 14856224768 | bytes 65429504 | tf_op jit(solution)/shard_map/recd,edf->recf/dot_general | solution.py:35
  332.2 34.5 %fusion.9 = bf16[8,7,46,1408]{3,2,0,1:T(8,128)(2,1)} fusion(f32[7,8,46,1408]{3,2,1,0:T(8,128)} %fusion.2, bf16[8,2048,1408]{2,1,0:T(8,128)(2,1)} %param.11, bf16[8,7,46,2048]{3,0,2,1:T(8,128)(2,1)} %bitcast.88), kind=kOutput, calls=%fused_computation.20 | convolution fusion | flops 14877986816 | bytes 73314304 | tf_op jit(solution)/shard_map/recd,edf->recf/dot_general | solution.py:34
  366.6 25.9 %convert_bitcast_fusion = bf16[8,7,46,2048]{3,2,0,1:T(8,128)(2,1)} fusion(bf16[8,7,46,1408]{3,2,0,1:T(8,128)(2,1)} %fusion.9, bf16[8,1408,2048]{2,1,0:T(8,128)(2,1)} %param.13), kind=kOutput, calls=%fused_computation.27 | convolution fusion | flops 14861500416 | bytes 58490880 | tf_op jit(solution)/shard_map/recf,efd->recd/dot_general | solution.py:37
  392.5 10.7 %copy.78 = bf16[8,7,46,2048]{3,0,2,1:T(8,128)(2,1)S(1)} copy(bf16[8,7,46,2048]{3,2,0,1:T(8,128)(2,1)} %convert_bitcast_fusion) | data formatting | bytes 21102592 | tf_op jit(solution)/shard_map/convert_element_type | solution.py:37
  403.2 0.0 copy-done.1
  403.2 5.7 pad_maximum_fusion
  408.9 19.0 %copy.80 = bf16[8,450,2048]{2,1,0:T(8,128)(2,1)} copy(bf16[8,450,2048]{2,0,1:T(8,128)(2,1)S(1)} %pad_maximum_fusion) | data formatting | bytes 29491200 | tf_op jit(solution)/shard_map/concatenate | solution.py:58
  427.9 5.9 all-to-all-start.1
  433.9 164.5 %all-to-all-done.1 = bf16[8,450,2048]{2,1,0:T(8,128)(2,1)} async-done(((bf16[8,450,2048]{2,1,0:T(8,128)(2,1)}), bf16[8,450,2048]{2,1,0:T(8,128)(2,1)}, u32[]{:S(2)}, u32[]{:S(2)}) %all-to-all-start.1) | async-done | bytes 14745632 | tf_op jit(solution)/shard_map/all_to_all | solution.py:59
  598.4 16.1 %reshape.146 = bf16[3600,2048]{1,0:T(8,128)(2,1)} reshape(bf16[8,450,2048]{2,1,0:T(8,128)(2,1)} %all-to-all-done.1) | data formatting | bytes 29491200 | tf_op jit(solution)/shard_map/reshape | solution.py:60
  614.6 9.4 %gather_fusion.6 = bf16[256,2048]{1,0:T(8,128)(2,1)S(1)} fusion(bf16[3600,2048]{1,0:T(8,128)(2,1)} %reshape.146, s32[1024]{0:T(1024)S(1)} %pad_clamp_fusion.1), kind=kCustom, calls=%fused_computation.6 | custom fusion | bytes 2098176 | tf_op jit(solution)/shard_map/gather | solution.py:29
  624.0 9.4 %gather_fusion.5 = bf16[256,2048]{1,0:T(8,128)(2,1)S(1)} fusion(bf16[3600,2048]{1,0:T(8,128)(2,1)} %reshape.146, s32[1024]{0:T(1024)S(1)} %pad_clamp_fusion.2), kind=kCustom, calls=%fused_computation.5 | custom fusion | bytes 2098176 | tf_op jit(solution)/shard_map/gather | solution.py:29
  633.5 9.4 %gather_fusion.4 = bf16[256,2048]{1,0:T(8,128)(2,1)S(1)} fusion(bf16[3600,2048]{1,0:T(8,128)(2,1)} %reshape.146, s32[1024]{0:T(1024)S(1)} %pad_clamp_fusion.3), kind=kCustom, calls=%fused_computation.4 | custom fusion | bytes 2098176 | tf_op jit(solution)/shard_map/gather | solution.py:29
  642.9 10.7 %gather_fusion.3 = bf16[256,2048]{1,0:T(8,128)(2,1)} fusion(bf16[3600,2048]{1,0:T(8,128)(2,1)} %reshape.146, s32[1024]{0:T(1024)S(1)} %pad_clamp_fusion.4), kind=kCustom, calls=%fused_computation.3 | custom fusion | bytes 2098176 | tf_op jit(solution)/shard_map/gather | solution.py:29
  653.6 10.4 %gather_fusion.2 = bf16[256,2048]{1,0:T(8,128)(2,1)} fusion(bf16[3600,2048]{1,0:T(8,128)(2,1)} %reshape.146, s32[1024]{0:T(1024)S(1)} %pad_clamp_fusion.5), kind=kCustom, calls=%fused_computation.2 | custom fusion | bytes 2098176 | tf_op jit(solution)/shard_map/gather | solution.py:29
  664.0 10.5 %gather_fusion.1 = bf16[256,2048]{1,0:T(8,128)(2,1)} fusion(bf16[3600,2048]{1,0:T(8,128)(2,1)} %reshape.146, s32[1024]{0:T(1024)S(1)} %pad_clamp_fusion.6), kind=kCustom, calls=%fused_computation.1 | custom fusion | bytes 2098176 | tf_op jit(solution)/shard_map/gather | solution.py:29
  674.5 4.1 add_convert_fusion
  (30 shorter events, 0.3 us)
Async XLA Ops:
  0.0 35.4 %copy-start.5 = (s32[256,6]{0,1:T(8,128)S(1)}, s32[256,6]{0,1:T(8,128)}, u32[]{:S(2)}) copy-start(s32[256,6]{0,1:T(8,128)} %param.8) | copy-start | bytes 18436
  0.0 42.0 %copy-start.2 = (bf16[256,2048]{1,0:T(8,128)(2,1)S(1)}, bf16[256,2048]{1,0:T(8,128)(2,1)}, u32[]{:S(2)}) copy-start(bf16[256,2048]{1,0:T(8,128)(2,1)} %param.7) | copy-start | bytes 3145732
  35.4 6.6 copy-start.3
  243.5 18.7 %copy-start = (bf16[8,450,2048]{2,1,0:T(8,128)(2,1)}, bf16[8,450,2048]{2,1,0:T(8,128)(2,1)S(1)}, u32[]{:S(2)}) copy-start(bf16[8,450,2048]{2,1,0:T(8,128)(2,1)S(1)} %all_to_all.10) | copy-start | bytes 44236804
  392.5 10.7 %copy-start.1 = (bf16[8,128,2048]{2,0,1:T(8,128)(2,1)S(1)}, bf16[8,128,2048]{2,0,1:T(8,128)(2,1)}, u32[]{:S(2)}) copy-start(bf16[8,128,2048]{2,0,1:T(8,128)(2,1)} %copy.79) | copy-start | bytes 12582916
  427.9 5.9 copy-start.4
  427.9 6.0 copy-start.6
  427.9 170.5 %all-to-all-start.1 = ((bf16[8,450,2048]{2,1,0:T(8,128)(2,1)}), bf16[8,450,2048]{2,1,0:T(8,128)(2,1)}, u32[]{:S(2)}, u32[]{:S(2)}) async-start(bf16[8,450,2048]{2,1,0:T(8,128)(2,1)} %copy.80), calls=%async_computation.1 | async-start | bytes 29884416 | tf_op jit(solution)/shard_map/all_to_all | solution.py:59
where the time goes:
time: 685 us; the launch traced here: 679 us
  local copies, waits for them, and re-layouts  185 us (27%)
  blocking collectives  170 us (25%)
  waiting for transfers between devices  164 us (24%)
  matrix products  124 us (18%)
  other arithmetic  29.2 us (4%)
    all_to_all x1, blocking collectives, local(): recv = lax.all_to_all(send, 'expert', 0, 0, tiled=True)  170 us
    all_to_all x1, waiting for transfers between devices, local(): back = lax.all_to_all(out, 'expert', 0, 0, tiled=True)  164 us
    gather x6, local copies, waits for them, and re-layouts, _combine(): y = y + g[:, j:j + 1] * back[dest[:, j]].astype(jnp.float32)  59.9 us
    dot_general x2, matrix products, _experts(): jnp.einsum(form_out, u, w2, preferred_element_type=jnp.float32)  48.6 us
    dot_general x2, matrix products, _experts(): b = jnp.einsum(form_in, xs, w3, preferred_element_type=jnp.float32)  40.8 us
    dot_general x1, matrix products, _experts(): a = jnp.einsum(form_in, xs, w1, preferred_element_type=jnp.float32)  34.5 us
    concatenate x1, local copies, waits for them, and re-layouts, local(): out = jnp.concatenate([out, oc.reshape(n, (el - 1) * cap, d)], axis=1)  19 us
    slice x2, local copies, waits for them, and re-layouts, local(): xc = recv[:, ch:].reshape(n, el - 1, cap, d)  18.7 us
  transfers between devices with their start and end apart: 1, of which 1 were waited for; matrix products, arithmetic and copies ran while one was open for 0% of the time, Pallas kernels for 0%

commit v1 on v0

v1 whole, which is shorter than its diff:
```python
import functools

import jax
import jax.numpy as jnp
from jax import lax
from jax.experimental import pallas as pl
from jax.experimental.pallas import tpu as pltpu
from jax.sharding import PartitionSpec as P

MESH = pl.DeviceIdType.MESH
F32 = jnp.float32
BF16 = jnp.bfloat16
CHIPS = 4
PIECES = 4
FC = 256
DC = 256


def _dot(a, b):
    return jnp.dot(a, b, preferred_element_type=F32)


def _iota(shape, dim):
    return lax.broadcasted_iota(jnp.int32, shape, dim)


def _kernel(cap, hot, x_hbm, ig_hbm, w1_hbm, w3_hbm, w2_hbm, out_ref,
            xall, mall, pos, u, uhot, pown, psib, drecv, frecv, nrecv,
            loc_sem, xsend_s, xsend_r, xsend_l, xrecv, msend, mrecv,
            wsem, w2sem, dsend, drs, fsend, frs, nsend, nrs):
    me = lax.axis_index('expert')
    n = 2 * CHIPS
    c, k = me // 2, me % 2

    def dev(o, kk):
        return ((c + o) % CHIPS) * 2 + kk

    sib, right, left, far = dev(0, 1 - k), dev(1, k), dev(3, k), dev(2, k)
    t, d = x_hbm.shape
    el, _, ff = w1_hbm.shape
    nf = ff // FC
    tail = ff - nf * FC
    extra = hot - cap
    nq = d // DC
    half = DC // 2
    pt = t // PIECES

    def remote(src, dst, ss, rs, to):
        return pltpu.make_async_remote_copy(src_ref=src, dst_ref=dst, send_sem=ss, recv_sem=rs,
                                            device_id={'expert': to}, device_id_type=MESH)

    def phase_up(xg, xhot, wbuf, wtail, pmat, tri):
        def w_copies(e, f):
            if f < nf:
                return [pltpu.make_async_copy(w.at[e, :, pl.ds(f * FC, FC)], wbuf.at[f, :, pl.ds(s * FC, FC)], wsem.at[f, s])
                        for s, w in enumerate((w1_hbm, w3_hbm))]
            return [pltpu.make_async_copy(w.at[e, :, pl.ds(nf * FC, tail)], wtail.at[:, pl.ds(s * tail, tail)], wsem.at[nf, s])
                    for s, w in enumerate((w1_hbm, w3_hbm))]

        own = pltpu.make_async_copy(x_hbm, xall.at[me], loc_sem.at[0])
        own_m = pltpu.make_async_copy(ig_hbm, mall.at[me], loc_sem.at[1])
        own.start()
        own_m.start()
        barrier = pltpu.get_barrier_semaphore()
        for peer in (sib, right, left):
            pl.semaphore_signal(barrier, inc=1, device_id={'expert': peer}, device_id_type=MESH)
        pl.semaphore_wait(barrier, 3)
        own.wait()
        own_m.wait()

        def piece(b, p, ss, to):
            rows = pl.ds(p * pt, pt)
            return remote(xall.at[b, rows], xall.at[b, rows], ss, xrecv.at[b, p], to)

        def meta(b, ss, to):
            return remote(mall.at[b], mall.at[b], ss, mrecv.at[b], to)

        sends = []

        def go(copy):
            copy.start()
            sends.append(copy)

        go(meta(me, msend.at[0], sib))
        go(meta(me, msend.at[1], right))
        go(meta(me, msend.at[2], left))
        for p in range(PIECES):
            q = (p + PIECES // 2) % PIECES
            go(piece(me, p, xsend_r.at[p], right))
            go(piece(me, q, xsend_l.at[q], left))
        for p in range(PIECES):
            go(piece(me, p, xsend_s.at[0, p], sib))
        for e_f in range(nf + 1):
            for cp in w_copies(0, e_f):
                cp.start()

        def got(b, p):
            piece(b, p, xsend_s.at[0, p], sib).wait_recv()

        def got_meta(b):
            meta(b, msend.at[0], sib).wait_recv()

        tri[...] = (_iota((t, t), 0) < _iota((t, t), 1)).astype(BF16)

        def gather(b):
            ids = mall[b, 0:8]
            gts = mall[b, 8:16]
            for e in range(el):
                eq = ids == (me * el + e).astype(F32)
                pos[0, b, e:e + 1, :] = jnp.sum(eq.astype(F32), axis=0, keepdims=True)
                pos[1, b, e:e + 1, :] = jnp.sum(jnp.where(eq, gts, 0.0), axis=0, keepdims=True)
            m = pos[0, b]
            before = _dot(m.astype(BF16), tri[...])
            rank = jnp.where(m > 0.0, before, -1.0)
            pos[0, b] = rank
            row = _iota((cap, t), 0).astype(F32)
            for e in range(el):
                pmat[e] = (rank[e:e + 1, :] == row).astype(BF16)
            sel = pmat[...].reshape(el * cap, t)

            def cols(j, _):
                w = pl.ds(pl.multiple_of(j * 512, 512), 512)
                r = _dot(sel, xall[b, :, w]).astype(BF16).reshape(el, cap, 512)
                for e in range(el):
                    xg[e, b, :, w] = r[e]
                return 0

            lax.fori_loop(0, d // 512, cols, 0)

            @pl.when(me == 0)
            def _():
                hrow = _iota((extra, t), 0).astype(F32) + float(cap)
                hsel = (rank[0:1, :] == hrow).astype(BF16)

                def hcols(j, _):
                    w = pl.ds(pl.multiple_of(j * 512, 512), 512)
                    xhot[b, :, w] = _dot(hsel, xall[b, :, w]).astype(BF16)
                    return 0

                lax.fori_loop(0, d // 512, hcols, 0)

        gather_later = []
        hp = PIECES // 2
        gather(me)
        got_meta(left)
        go(meta(left, msend.at[3], right))
        go(meta(left, msend.at[4], sib))
        got_meta(right)
        go(meta(right, msend.at[5], sib))
        for p in range(hp):
            got(left, p)
            go(piece(left, p, xsend_r.at[PIECES + p], right))
            go(piece(left, p, xsend_s.at[1, p], sib))
            got(right, hp + p)
            go(piece(right, hp + p, xsend_l.at[PIECES + p], left))
            go(piece(right, hp + p, xsend_s.at[2, hp + p], sib))
        for p in range(hp):
            got(left, hp + p)
            go(piece(left, hp + p, xsend_s.at[1, hp + p], sib))
            got(right, p)
            go(piece(right, p, xsend_s.at[2, p], sib))

        def rest(b):
            got_meta(b)
            for p in range(PIECES):
                got(b, p)
            gather(b)

        gather(left)
        gather(right)
        rest(sib)
        got_meta(far)
        go(meta(far, msend.at[6], sib))
        for p in range(hp):
            got(far, p)
            go(piece(far, p, xsend_s.at[3, p], sib))
            got(far, hp + p)
            go(piece(far, hp + p, xsend_s.at[3, hp + p], sib))
        rest(dev(3, 1 - k))
        rest(dev(1, 1 - k))
        gather(far)
        rest(dev(2, 1 - k))

        def up(e, _):
            lhs = xg[e].reshape(n * cap, d)

            def act(rows, w, width):
                ab = _dot(rows, w)
                a, b = ab[:, :width], ab[:, width:]
                return (a * jax.nn.sigmoid(a) * b).astype(BF16)

            for f in range(nf + 1):
                for cp in w_copies(e, f):
                    cp.wait()
                w_ref, width = (wbuf.at[f], FC) if f < nf else (wtail, tail)
                w_cols = pl.ds(f * FC, width)
                u[e, :, w_cols] = act(lhs, w_ref[...], width)

                @pl.when(jnp.logical_and(me == 0, e == 0))
                def _():
                    hr = n * extra // 2
                    for s in range(2):
                        rows = xhot[s * (n // 2):(s + 1) * (n // 2)].reshape(hr, d)
                        uhot[s * hr:(s + 1) * hr, w_cols] = act(rows, w_ref[...], width)

                @pl.when(e + 1 < el)
                def _():
                    for cp in w_copies(jnp.minimum(e + 1, el - 1), f):
                        cp.start()
            return 0

        lax.fori_loop(0, el, up, 0)
        for copy in sends:
            copy.wait_send()

    pl.run_scoped(phase_up,
                  pltpu.VMEM((el, n, cap, d), BF16), pltpu.VMEM((n, extra, d), BF16),
                  pltpu.VMEM((nf, d, 2 * FC), BF16), pltpu.VMEM((d, 2 * tail), BF16),
                  pltpu.VMEM((el, cap, t), BF16), pltpu.VMEM((t, t), BF16))

    def phase_down(w2buf, s_all, s_hot, hbuf, hhot, cat):
        def w2_copy(q, e):
            cols = pl.ds(pl.multiple_of(q * DC, DC), DC)
            return pltpu.make_async_copy(w2_hbm.at[e, :, cols], w2buf.at[e], w2sem.at[e])

        for e in range(el):
            w2_copy(0, e).start()

        for b in range(n):
            cat[b * el:(b + 1) * el, :] = pos[0, b]
            cat[(n + b) * el:(n + b + 1) * el, :] = pos[1, b]
        cols = jnp.transpose(cat[...])
        g1 = cols.astype(BF16)
        r1 = cols - g1.astype(F32)
        g2 = r1.astype(BF16)
        g3 = (r1 - g2.astype(F32)).astype(BF16)
        lane = _iota((1, el * cap), 1)
        slot_e = jnp.zeros((1, el * cap), jnp.int32)
        for e in range(1, el):
            slot_e = slot_e + (lane >= e * cap).astype(jnp.int32)
        want = (lane - cap * slot_e).astype(F32)

        def build(b, _):
            rr = _iota((2 * n * el, el * cap), 0)
            lo = (rr - b * el) * cap
            ll = _iota((2 * n * el, el * cap), 1)
            pick = jnp.logical_and(ll >= lo, ll < lo + cap).astype(BF16)
            lo2 = lo - n * el * cap
            pick2 = jnp.logical_and(ll >= lo2, ll < lo2 + cap).astype(BF16)
            hit = _dot(g1, pick) == want
            for s, gs in enumerate((g1, g2, g3)):
                s_all[b, s] = jnp.where(hit, _dot(gs, pick2), 0.0).astype(BF16)

            @pl.when(me == 0)
            def _():
                rh = _iota((2 * n * el, extra), 0)
                hpick = (rh == b * el).astype(BF16)
                hpick2 = (rh == (n + b) * el).astype(BF16)
                hhit = _dot(g1, hpick) == (_iota((t, extra), 1) + cap).astype(F32)
                for s, gs in enumerate((g1, g2, g3)):
                    s_hot[b, s] = jnp.where(hhit, _dot(gs, hpick2), 0.0).astype(BF16)

            return 0

        lax.fori_loop(0, n, build, 0)

        def d_copy(q):
            return remote(psib.at[q % 2], drecv.at[q % 2], dsend.at[q % 2], drs.at[q % 2], sib)

        def f_copies(q):
            return [remote(pown.at[q % 4, 2, s], frecv.at[q % 2, s], fsend.at[q % 4, s], frs.at[q % 2, s], to)
                    for s, to in enumerate((right, left))]

        def n_copies(q):
            return [remote(pown.at[q % 4, o], nrecv.at[q % 2, s], nsend.at[q % 4, s], nrs.at[q % 2, s], to)
                    for s, (o, to) in enumerate(((1, right), (3, left)))]

        def step(i, _):
            @pl.when(i >= 3)
            def _():
                q = i - 3
                for cp in n_copies(q):
                    cp.wait_recv()
                for s in range(2):
                    y = pown[q % 4, 0, s] + nrecv[q % 2, 0, s] + nrecv[q % 2, 1, s]
                    out_ref[:, pl.ds(pl.multiple_of(q * DC + s * half, half), half)] = y.astype(BF16)

            @pl.when(jnp.logical_and(i >= 1, i <= nq))
            def _():
                q = i - 1
                d_copy(q).wait_recv()
                for o in (2, 1, 3, 0):
                    pown[q % 4, o] = pown[q % 4, o] + drecv[q % 2, o]
                for cp in f_copies(q):
                    cp.start()

            @pl.when(jnp.logical_and(i >= 2, i <= nq + 1))
            def _():
                q = i - 2
                for cp in f_copies(q):
                    cp.wait_recv()
                pown[q % 4, 1, 0] = pown[q % 4, 1, 0] + frecv[q % 2, 0]
                pown[q % 4, 3, 1] = pown[q % 4, 3, 1] + frecv[q % 2, 1]
                for cp in n_copies(q):
                    cp.start()

            @pl.when(i < nq)
            def _():
                q = i

                def down(e, _):
                    w2_copy(q, e).wait()
                    h = _dot(u[e], w2buf[e]).astype(BF16).reshape(n, cap, DC)
                    for b in range(n):
                        hbuf[b, e] = h[b]

                    @pl.when(jnp.logical_and(me == 0, e == 0))
                    def _():
                        hhot[...] = _dot(uhot[...], w2buf[e]).astype(BF16).reshape(n, extra, DC)

                    @pl.when(q + 1 < nq)
                    def _():
                        w2_copy(jnp.minimum(q + 1, nq - 1), e).start()

                    return 0

                lax.fori_loop(0, el, down, 0)

                @pl.when(i >= 4)
                def _():
                    for cp in f_copies(q - 4) + n_copies(q - 4):
                        cp.wait_send()

                @pl.when(i >= 2)
                def _():
                    d_copy(q - 2).wait_send()

                def scatter(o, _):
                    for kk, dst in ((1 - k, psib.at[q % 2, o]), (k, pown.at[q % 4, o])):
                        b = dev(o, kk)
                        r = _dot(s_all[b].reshape(3 * t, el * cap), hbuf[b].reshape(el * cap, DC))
                        r = r[:t] + r[t:2 * t] + r[2 * t:]
                        dst[0] = r[:, :half]
                        dst[1] = r[:, half:]

                        @pl.when(me == 0)
                        def _():
                            z = _dot(s_hot[b].reshape(3 * t, extra), hhot[b])
                            z = z[:t] + z[t:2 * t] + z[2 * t:]
                            dst[0] = dst[0] + z[:, :half]
                            dst[1] = dst[1] + z[:, half:]

                    return 0

                lax.fori_loop(0, CHIPS, scatter, 0)
                d_copy(q).start()

            return 0

        lax.fori_loop(0, nq + 3, step, 0)
        for q in range(nq - 4, nq):
            for cp in f_copies(q) + n_copies(q):
                cp.wait_send()
        for q in range(nq - 2, nq):
            d_copy(q).wait_send()

    pl.run_scoped(phase_down,
                  pltpu.VMEM((el, ff, DC), BF16), pltpu.VMEM((n, 3, t, el * cap), BF16),
                  pltpu.VMEM((n, 3, t, extra), BF16), pltpu.VMEM((n, el, cap, DC), BF16),
                  pltpu.VMEM((n, extra, DC), BF16), pltpu.VMEM((2 * n * el, t), F32))


def solution(mesh):
    n = mesh.shape['expert']
    assert n == 2 * CHIPS

    def local(x, idx, g, hot_tok, w1, w3, w2):
        t, d = x.shape
        k = idx.shape[1]
        el, _, ff = w1.shape
        e = el * n
        hot = hot_tok.shape[0]
        most = 2 * ((t * k - hot + e - 2) // (e - 1))
        cap = -(-most // 16) * 16
        extra = hot - cap
        half = DC // 2
        pad = jnp.full((8 - k, t), -1.0, F32)
        ig = jnp.concatenate([idx.T.astype(F32), pad, g.T, pad])
        dma, any_ = pltpu.SemaphoreType.DMA, pl.BlockSpec(memory_space=pl.ANY)
        return pl.pallas_call(
            functools.partial(_kernel, cap, hot),
            out_shape=jax.ShapeDtypeStruct((t, d), BF16),
            in_specs=[any_] * 5,
            out_specs=pl.BlockSpec(memory_space=pltpu.VMEM),
            scratch_shapes=[
                pltpu.VMEM((n, t, d), BF16), pltpu.VMEM((n, 16, t), F32), pltpu.VMEM((2, n, el, t), F32),
                pltpu.VMEM((el, n * cap, ff), BF16), pltpu.VMEM((n * extra, ff), BF16),
                pltpu.VMEM((4, CHIPS, 2, t, half), F32), pltpu.VMEM((2, CHIPS, 2, t, half), F32),
                pltpu.VMEM((2, CHIPS, 2, t, half), F32), pltpu.VMEM((2, 2, t, half), F32),
                pltpu.VMEM((2, 2, 2, t, half), F32),
                dma((2,)), dma((4, PIECES)), dma((2 * PIECES,)), dma((2 * PIECES,)), dma((n, PIECES)), dma((7,)), dma((n,)),
                dma((ff // FC + 1, 2)), dma((el,)), dma((2,)), dma((2,)), dma((4, 2)), dma((2, 2)), dma((4, 2)), dma((2, 2)),
            ],
            compiler_params=pltpu.CompilerParams(collective_id=0, has_side_effects=True, vmem_limit_bytes=67043328),
        )(x, ig, w1, w3, w2)

    rows = P(('data', 'expert'))
    wspec = P('expert')
    return jax.shard_map(local, mesh=mesh, in_specs=(rows, rows, rows, rows, wspec, wspec, wspec), out_specs=rows, check_vma=False)
```

time: 685 us -> 220 us (0.32)
  Pallas kernels: 0 us -> 215 us
  local copies, waits for them, and re-layouts: 185 us -> 2.31 us
  blocking collectives: 170 us -> 0 us
  waiting for transfers between devices: 164 us -> 0 us
  matrix products: 124 us -> 0 us
  other arithmetic: 29.2 us -> 2.01 us
    pallas_call x0 -> x1, Pallas kernels: none -> 215 us  [local(): pl.pallas_call(functools.partial(_kernel, cap, hot), out_shape=jax.ShapeD...]
    all_to_all x1 -> x0, blocking collectives: 170 us -> none  [local(): recv = lax.all_to_all(send, 'expert', 0, 0, tiled=True)]
    all_to_all x1 -> x0, waiting for transfers between devices: 164 us -> none  [local(): back = lax.all_to_all(out, 'expert', 0, 0, tiled=True)]
    dot_general x5 -> x0, matrix products: 124 us -> none  [the longest x2 48.6 us: _experts(): jnp.einsum(form_out, u, w2, preferred_element_type=jnp.float32)]
    gather x10 -> x0, local copies, waits for them, and re-layouts: 88 us -> none  [the longest x6 59.9 us: _combine(): y = y + g[:, j:j + 1] * back[dest[:, j]].astype(jnp.float32)]
    reshape x4 -> x0, local copies, waits for them, and re-layouts: 32.5 us -> none  [the longest x1 16.1 us: local(): return _combine(back.reshape(n * s, d), dest, g)]
    slice x5 -> x0, local copies, waits for them, and re-layouts: 19.2 us -> none  [the longest x2 18.7 us: local(): xc = recv[:, ch:].reshape(n, el - 1, cap, d)]
    concatenate x2 -> x0, local copies, waits for them, and re-layouts: 19.1 us -> none  [the longest x1 19 us: local(): out = jnp.concatenate([out, oc.reshape(n, (el - 1) * cap, d)], axis=1)]
  transfers between devices with their start and end apart: 1 -> 0, of which waited for: 1 -> 0; matrix products, arithmetic and copies ran while one was open for 0% -> 0% of each run, Pallas kernels for 0% -> 0%
where the time goes in v1:
time: 220 us
  Pallas kernels  215 us (98%)
  local copies, waits for them, and re-layouts  2.31 us (1%)
    pallas_call x1, Pallas kernels, local(): pl.pallas_call(functools.partial(_kernel, cap, hot), out_shape=jax.ShapeD...  215 us

profile of v1, /device:TPU:112, one launch (start us, length us, event | category | flops | bytes accessed | tf_op | source)
XLA Modules:
  0.0 219.7 jit_solution(2355227956827676941)
XLA Ops:
  0.0 0.7 convert_bitcast_fusion
  0.7 1.3 pad_maximum_fusion.ig_hbm
  2.0 215.4 %shard_map.64 = bf16[256,2048]{1,0:T(8,128)(2,1)} custom-call(bf16[256,2048]{1,0:T(8,128)(2,1)} %x_hbm.1, f32[16,256]{1,0:T(8,128)} %pad_maximum_fusion.ig_hbm, bf16[8,2048,1408]{2,1,0:T(8,128)(2,1)} %w1_hbm.1, bf16[8,2048,1408]{2,1,0:T(8,128)(2,1)} %w3_hbm.1, bf16[8,1408,2048]{2,1,0:T(8,128)(2,1)} %w2_hbm.1), custom_call_target="tpu_custom_call" | custom-call | tf_op jit(solution)/shard_map/pallas_call | solution.py:390
  217.4 2.3 %copy.8 = bf16[256,2048]{1,0:T(8,128)(2,1)} copy(bf16[256,2048]{1,0:T(8,128)(2,1)} %shard_map.64) | data formatting | bytes 2097152
  (1 shorter events, 0.0 us)

commit v2 on v0

v2 whole, which is shorter than its diff:
```python
import functools

import jax
import jax.numpy as jnp
from jax import lax
from jax.experimental import pallas as pl
from jax.experimental.pallas import tpu as pltpu
from jax.sharding import PartitionSpec as P

MESH = pl.DeviceIdType.MESH
F32 = jnp.float32
BF16 = jnp.bfloat16
CHIPS = 4
PIECES = 4
FC = 256
DC = 256


def _dot(a, b):
    return jnp.dot(a, b, preferred_element_type=F32)


def _iota(shape, dim):
    return lax.broadcasted_iota(jnp.int32, shape, dim)


def _kernel(cap, hot, x_hbm, ig_hbm, w1_hbm, w3_hbm, w2_hbm, out_ref,
            xall, mall, pos, xg, xhot, u, uhot, wbuf, wtail, w2buf, s_all, s_hot, hbuf, hhot,
            pown, psib, drecv, frecv, nrecv, cat, pmat, tri,
            loc_sem, xsend_s, xsend_r, xsend_l, xrecv, msend, mrecv,
            wsem, w2sem, dsend, drs, fsend, frs, nsend, nrs, credit):
    me = lax.axis_index('expert')
    c, k = me // 2, me % 2

    def dev(o, kk):
        return ((c + o) % CHIPS) * 2 + kk

    sib, right, left, far = dev(0, 1 - k), dev(1, k), dev(3, k), dev(2, k)
    t, d = x_hbm.shape
    el, _, ff = w1_hbm.shape
    nf = ff // FC
    tail = ff - nf * FC
    extra = hot - cap
    nq = d // DC
    half = DC // 2
    pt = t // PIECES
    hp = PIECES // 2
    rows = CHIPS * cap

    def remote(src, dst, ss, rs, to):
        return pltpu.make_async_remote_copy(src_ref=src, dst_ref=dst, send_sem=ss, recv_sem=rs,
                                            device_id={'expert': to}, device_id_type=MESH)

    def w_copies(e, f):
        if f < nf:
            return [pltpu.make_async_copy(w.at[e, :, pl.ds(f * FC, FC)], wbuf.at[f, :, pl.ds(s * FC, FC)], wsem.at[f, s])
                    for s, w in enumerate((w1_hbm, w3_hbm))]
        return [pltpu.make_async_copy(w.at[e, :, pl.ds(nf * FC, tail)], wtail.at[:, pl.ds(s * tail, tail)], wsem.at[nf, s])
                for s, w in enumerate((w1_hbm, w3_hbm))]

    def w2_copy(q, e):
        cols = pl.ds(pl.multiple_of(q * DC, DC), DC)
        return pltpu.make_async_copy(w2_hbm.at[e, :, cols], w2buf.at[e], w2sem.at[e])

    def piece(b, p, ss, to):
        r = pl.ds(p * pt, pt)
        return remote(xall.at[b, r], xall.at[b, r], ss, xrecv.at[b, p], to)

    def meta(b, ss, to):
        return remote(mall.at[b], mall.at[b], ss, mrecv.at[b], to)

    def got(b, p):
        piece(b, p, xsend_s.at[0, p], sib).wait_recv()

    def got_meta(b):
        meta(b, msend.at[0], sib).wait_recv()

    def to_sib(o, p):
        return piece(dev(o, k), p, xsend_s.at[o, p], sib)

    def own_right(p):
        return piece(me, p, xsend_r.at[p], right)

    def own_left(p):
        return piece(me, p, xsend_l.at[p], left)

    def relay_right(p):
        return piece(left, p, xsend_r.at[PIECES + p], right)

    def relay_left(p):
        return piece(right, hp + p, xsend_l.at[PIECES + p], left)

    def token_sends():
        out = [to_sib(o, p) for o in range(CHIPS) for p in range(PIECES)]
        out += [own_right(p) for p in range(PIECES)] + [own_left(p) for p in range(PIECES)]
        return out + [relay_right(p) for p in range(hp)] + [relay_left(p) for p in range(hp)]

    def send_own():
        for p in range(PIECES):
            own_right(p).start()
            own_left((p + hp) % PIECES).start()
        for p in range(PIECES):
            to_sib(0, p).start()

    def relay(p):
        got(left, p)
        relay_right(p).start()
        got(right, hp + p)
        relay_left(p).start()

    def sib_near(first):
        for p in range(hp):
            q = p if first else hp + p
            to_sib(3, q).start()
            to_sib(1, hp + p if first else p).start()

    def rest_near():
        for p in range(hp):
            got(left, hp + p)
            got(right, p)

    def far_in():
        for p in range(hp):
            got(far, p)
            to_sib(2, p).start()
            got(far, hp + p)
            to_sib(2, hp + p).start()

    def wait_block(b):
        for p in range(PIECES):
            got(b, p)

    def gather(beta, o):
        b = dev(o, beta)
        ids = mall[b, 0:8]
        gts = mall[b, 8:16]
        for e in range(el):
            eq = ids == (me * el + e).astype(F32)
            pos[0, o, e:e + 1, :] = jnp.sum(eq.astype(F32), axis=0, keepdims=True)
            pos[1, o, e:e + 1, :] = jnp.sum(jnp.where(eq, gts, 0.0), axis=0, keepdims=True)
        m = pos[0, o]
        before = _dot(m.astype(BF16), tri[...])
        rank = jnp.where(m > 0.0, before, -1.0)
        pos[0, o] = rank
        row = _iota((cap, t), 0).astype(F32)
        for e in range(el):
            pmat[e] = (rank[e:e + 1, :] == row).astype(BF16)
        sel = pmat[...].reshape(el * cap, t)

        def cols(j, _):
            w = pl.ds(pl.multiple_of(j * 512, 512), 512)
            r = _dot(sel, xall[b, :, w]).astype(BF16).reshape(el, cap, 512)
            for e in range(el):
                xg[e, o, :, w] = r[e]
            return 0

        lax.fori_loop(0, d // 512, cols, 0)

        @pl.when(me == 0)
        def _():
            hrow = _iota((extra, t), 0).astype(F32) + float(cap)
            hsel = (rank[0:1, :] == hrow).astype(BF16)

            def hcols(j, _):
                w = pl.ds(pl.multiple_of(j * 512, 512), 512)
                xhot[o, :, w] = _dot(hsel, xall[b, :, w]).astype(BF16)
                return 0

            lax.fori_loop(0, d // 512, hcols, 0)

    def up(beta, hook):
        def body(i, _):
            e = i if beta == 0 else el - 1 - i
            after = jnp.minimum(e + 1, el - 1) if beta == 0 else jnp.maximum(e - 1, 0)
            hook(i)
            lhs = xg[e].reshape(rows, d)

            def act(r, w, width):
                ab = _dot(r, w)
                a, b = ab[:, :width], ab[:, width:]
                return (a * jax.nn.sigmoid(a) * b).astype(BF16)

            for f in range(nf + 1):
                if beta == 0:
                    for cp in w_copies(e, f):
                        cp.wait()
                else:
                    @pl.when(i > 0)
                    def _():
                        for cp in w_copies(e, f):
                            cp.wait()
                w_ref, width = (wbuf.at[f], FC) if f < nf else (wtail, tail)
                w_cols = pl.ds(f * FC, width)
                u[e, :, w_cols] = act(lhs, w_ref[...], width)

                @pl.when(jnp.logical_and(me == 0, e == 0))
                def _():
                    uhot[:, w_cols] = act(xhot[...].reshape(CHIPS * extra, d), w_ref[...], width)

                @pl.when(i + 1 < el)
                def _():
                    for cp in w_copies(after, f):
                        cp.start()
            return 0

        lax.fori_loop(0, el, body, 0)

    def d_copy(q):
        return remote(psib.at[q % 2], drecv.at[q % 2], dsend.at[q % 2], drs.at[q % 2], sib)

    def f_copies(q):
        return [remote(pown.at[q, 2, s], frecv.at[q, s], fsend.at[q, s], frs.at[q, s], to)
                for s, to in enumerate((right, left))]

    def n_copies(q):
        return [remote(pown.at[q, o], nrecv.at[q, s], nsend.at[q, s], nrs.at[q, s], to)
                for s, (o, to) in enumerate(((1, right), (3, left)))]

    def pair_add(q):
        d_copy(q).wait_recv()
        for o in (2, 1, 3, 0):
            pown[q, o] = psib[q % 2, o] + drecv[q % 2, o]
        for cp in f_copies(q):
            cp.start()

        @pl.when(q < nq - 2)
        def _():
            pl.semaphore_signal(credit, inc=1, device_id={'expert': sib}, device_id_type=MESH)

    def relay_add(q):
        for cp in f_copies(q):
            cp.wait_recv()
        pown[q, 1, 0] = pown[q, 1, 0] + frecv[q, 0]
        pown[q, 3, 1] = pown[q, 3, 1] + frecv[q, 1]
        for cp in n_copies(q):
            cp.start()

    def finish(q, _):
        for cp in n_copies(q):
            cp.wait_recv()
        for s in range(2):
            y = pown[q, 0, s] + nrecv[q, 0, s] + nrecv[q, 1, s]
            out_ref[:, pl.ds(pl.multiple_of(q * DC + s * half, half), half)] = y.astype(BF16)
        return 0

    def build_scatter():
        cat[...] = jnp.zeros_like(cat)
        for o in range(CHIPS):
            cat[o * el:(o + 1) * el, :] = pos[0, o]
            cat[(CHIPS + o) * el:(CHIPS + o + 1) * el, :] = pos[1, o]
        cols = jnp.transpose(cat[...])
        g1 = cols.astype(BF16)
        r1 = cols - g1.astype(F32)
        g2 = r1.astype(BF16)
        g3 = (r1 - g2.astype(F32)).astype(BF16)
        lane = _iota((1, el * cap), 1)
        slot_e = jnp.zeros((1, el * cap), jnp.int32)
        for e in range(1, el):
            slot_e = slot_e + (lane >= e * cap).astype(jnp.int32)
        want = (lane - cap * slot_e).astype(F32)
        depth = cat.shape[0]

        def build(o, _):
            rr = _iota((depth, el * cap), 0)
            ll = _iota((depth, el * cap), 1)
            lo = (rr - o * el) * cap
            pick = jnp.logical_and(ll >= lo, ll < lo + cap).astype(BF16)
            lo2 = lo - CHIPS * el * cap
            pick2 = jnp.logical_and(ll >= lo2, ll < lo2 + cap).astype(BF16)
            hit = _dot(g1, pick) == want
            for s, gs in enumerate((g1, g2, g3)):
                s_all[o, s] = jnp.where(hit, _dot(gs, pick2), 0.0).astype(BF16)

            @pl.when(me == 0)
            def _():
                rh = _iota((depth, extra), 0)
                hpick = (rh == o * el).astype(BF16)
                hpick2 = (rh == (CHIPS + o) * el).astype(BF16)
                hhit = _dot(g1, hpick) == (_iota((t, extra), 1) + cap).astype(F32)
                for s, gs in enumerate((g1, g2, g3)):
                    s_hot[o, s] = jnp.where(hhit, _dot(gs, hpick2), 0.0).astype(BF16)

            return 0

        lax.fori_loop(0, CHIPS, build, 0)

    def chunk(beta, q):
        def down(e, _):
            w2_copy(q, e).wait()
            h = _dot(u[e], w2buf[e]).astype(BF16).reshape(CHIPS, cap, DC)
            for o in range(CHIPS):
                hbuf[o, e] = h[o]

            @pl.when(jnp.logical_and(me == 0, e == 0))
            def _():
                hhot[...] = _dot(uhot[...], w2buf[e]).astype(BF16).reshape(CHIPS, extra, DC)

            if beta == 0:
                w2_copy((q + 1) % nq, e).start()
            else:
                @pl.when(q + 1 < nq)
                def _():
                    w2_copy(jnp.minimum(q + 1, nq - 1), e).start()

            return 0

        lax.fori_loop(0, el, down, 0)

        @pl.when(jnp.logical_and(k != beta, q >= 2))
        def _():
            d_copy(q - 2).wait_send()

        def scatter(o, _):
            r = _dot(s_all[o].reshape(3 * t, el * cap), hbuf[o].reshape(el * cap, DC))
            r = r[:t] + r[t:2 * t] + r[2 * t:]
            psib[q % 2, o, 0] = r[:, :half]
            psib[q % 2, o, 1] = r[:, half:]

            @pl.when(me == 0)
            def _():
                z = _dot(s_hot[o].reshape(3 * t, extra), hhot[o])
                z = z[:t] + z[t:2 * t] + z[2 * t:]
                psib[q % 2, o, 0] = psib[q % 2, o, 0] + z[:, :half]
                psib[q % 2, o, 1] = psib[q % 2, o, 1] + z[:, half:]

            return 0

        lax.fori_loop(0, CHIPS, scatter, 0)

        @pl.when(k != beta)
        def _():
            @pl.when(q >= 2)
            def _():
                pl.semaphore_wait(credit, 1)
            d_copy(q).start()

    def down_phase(beta):
        build_scatter()
        last = nq + 1 if beta == 0 else nq + 3

        def step(i, _):
            @pl.when(jnp.logical_and(k == beta, jnp.logical_and(i >= 1, i <= nq)))
            def _():
                pair_add(i - 1)

            if beta == 0:
                for at, q in ((3, 0), (5, 1), (7, 2)):
                    @pl.when(jnp.logical_and(k == beta, i == at))
                    def _():
                        relay_add(q)
            else:
                @pl.when(jnp.logical_and(k == beta, i >= 3))
                def _():
                    relay_add(i - 3)

            @pl.when(i < nq)
            def _():
                chunk(beta, i)

            return 0

        lax.fori_loop(0, last, step, 0)

        @pl.when(k != beta)
        def _():
            for q in range(nq - 2, nq):
                d_copy(q).wait_send()

    own = pltpu.make_async_copy(x_hbm, xall.at[me], loc_sem.at[0])
    own_m = pltpu.make_async_copy(ig_hbm, mall.at[me], loc_sem.at[1])
    own.start()
    own_m.start()
    barrier = pltpu.get_barrier_semaphore()
    for peer in (sib, right, left):
        pl.semaphore_signal(barrier, inc=1, device_id={'expert': peer}, device_id_type=MESH)
    pl.semaphore_wait(barrier, 3)
    own.wait()
    own_m.wait()
    metas = [meta(me, msend.at[0], sib), meta(me, msend.at[1], right), meta(me, msend.at[2], left)]
    for cp in metas:
        cp.start()

    @pl.when(k == 0)
    def _():
        send_own()

    for f in range(nf + 1):
        for cp in w_copies(0, f):
            cp.start()
    for e in range(el):
        w2_copy(0, e).start()
    tri[...] = (_iota((t, t), 0) < _iota((t, t), 1)).astype(BF16)

    got_meta(left)
    metas += [meta(left, msend.at[3], right), meta(left, msend.at[4], sib)]
    metas[3].start()
    metas[4].start()
    got_meta(right)
    metas += [meta(right, msend.at[5], sib)]
    metas[5].start()
    got_meta(far)
    metas += [meta(far, msend.at[6], sib)]
    metas[6].start()
    for o in range(CHIPS):
        got_meta(dev(o, 1 - k))

    @pl.when(k == 1)
    def _():
        wait_block(dev(0, 0))

    gather(0, 0)

    @pl.when(k == 0)
    def _():
        for p in range(hp):
            relay(p)
        sib_near(True)
        rest_near()
        sib_near(False)

    @pl.when(k == 1)
    def _():
        wait_block(dev(3, 0))
        wait_block(dev(1, 0))

    gather(0, 3)
    gather(0, 1)

    @pl.when(k == 0)
    def _():
        far_in()

    @pl.when(k == 1)
    def _():
        wait_block(dev(2, 0))
        send_own()

    gather(0, 2)

    def hook_first(i):
        @pl.when(k == 1)
        def _():
            for at, p in ((1, 0), (2, 1)):
                @pl.when(i == at)
                def _():
                    relay(p)

            @pl.when(i == 4)
            def _():
                rest_near()
                sib_near(True)
                sib_near(False)

            @pl.when(i == 6)
            def _():
                far_in()

    up(0, hook_first)
    down_phase(0)

    @pl.when(k == 0)
    def _():
        for o in range(CHIPS):
            wait_block(dev(o, 1))

    for o in range(CHIPS):
        gather(1, o)

    def hook_second(i):
        @pl.when(jnp.logical_and(k == 0, i < nq - 3))
        def _():
            relay_add(3 + i)

    up(1, hook_second)
    down_phase(1)
    lax.fori_loop(0, nq, finish, 0)

    for cp in metas:
        cp.wait_send()
    for cp in token_sends():
        cp.wait_send()
    for q in range(nq):
        for cp in f_copies(q) + n_copies(q):
            cp.wait_send()


def solution(mesh):
    n = mesh.shape['expert']
    assert n == 2 * CHIPS

    def local(x, idx, g, hot_tok, w1, w3, w2):
        t, d = x.shape
        k = idx.shape[1]
        el, _, ff = w1.shape
        e = el * n
        hot = hot_tok.shape[0]
        most = 2 * ((t * k - hot + e - 2) // (e - 1))
        cap = -(-most // 16) * 16
        extra = hot - cap
        half = DC // 2
        nf, nq = ff // FC, d // DC
        tail = ff - nf * FC
        pad = jnp.full((8 - k, t), -1.0, F32)
        ig = jnp.concatenate([idx.T.astype(F32), pad, g.T, pad])
        dma, any_ = pltpu.SemaphoreType.DMA, pl.BlockSpec(memory_space=pl.ANY)
        vm = pltpu.VMEM
        return pl.pallas_call(
            functools.partial(_kernel, cap, hot),
            out_shape=jax.ShapeDtypeStruct((t, d), BF16),
            in_specs=[any_] * 5,
            out_specs=pl.BlockSpec(memory_space=pltpu.VMEM),
            scratch_shapes=[
                vm((n, t, d), BF16), vm((n, 16, t), F32), vm((2, CHIPS, el, t), F32),
                vm((el, CHIPS, cap, d), BF16), vm((CHIPS, extra, d), BF16),
                vm((el, CHIPS * cap, ff), BF16), vm((CHIPS * extra, ff), BF16),
                vm((nf, d, 2 * FC), BF16), vm((d, 2 * tail), BF16), vm((el, ff, DC), BF16),
                vm((CHIPS, 3, t, el * cap), BF16), vm((CHIPS, 3, t, extra), BF16),
                vm((CHIPS, el, cap, DC), BF16), vm((CHIPS, extra, DC), BF16),
                vm((nq, CHIPS, 2, t, half), F32), vm((2, CHIPS, 2, t, half), F32), vm((2, CHIPS, 2, t, half), F32),
                vm((nq, 2, t, half), F32), vm((nq, 2, 2, t, half), F32),
                vm((-(-2 * CHIPS * el // 128) * 128, t), F32), vm((el, cap, t), BF16), vm((t, t), BF16),
                dma((2,)), dma((CHIPS, PIECES)), dma((2 * PIECES,)), dma((2 * PIECES,)), dma((n, PIECES)), dma((7,)), dma((n,)),
                dma((nf + 1, 2)), dma((el,)), dma((2,)), dma((2,)), dma((nq, 2)), dma((nq, 2)), dma((nq, 2)), dma((nq, 2)),
                pltpu.SemaphoreType.REGULAR,
            ],
            compiler_params=pltpu.CompilerParams(collective_id=0, has_side_effects=True, vmem_limit_bytes=67043328),
        )(x, ig, w1, w3, w2)

    rows = P(('data', 'expert'))
    wspec = P('expert')
    return jax.shard_map(local, mesh=mesh, in_specs=(rows, rows, rows, rows, wspec, wspec, wspec), out_specs=rows, check_vma=False)
```

time: 685 us -> 218 us (0.32)
  the two profiles are of different devices: /device:TPU:112 before, /device:TPU:113 now
where the time goes in v2:
time: 218 us; the launch traced here: 217 us
  Pallas kernels  213 us (98%)
  local copies, waits for them, and re-layouts  2.31 us (1%)
    pallas_call x1, Pallas kernels, local(): pl.pallas_call(functools.partial(_kernel, cap, hot), out_shape=jax.ShapeD...  213 us

profile of v2, /device:TPU:113, one launch (start us, length us, event | category | flops | bytes accessed | tf_op | source)
XLA Modules:
  0.0 217.5 jit_solution(14743490253670453188)
XLA Ops:
  0.0 0.7 convert_bitcast_fusion
  0.7 1.3 pad_maximum_fusion.ig_hbm
  2.0 213.1 %shard_map.64 = bf16[256,2048]{1,0:T(8,128)(2,1)} custom-call(bf16[256,2048]{1,0:T(8,128)(2,1)} %x_hbm.1, f32[16,256]{1,0:T(8,128)} %pad_maximum_fusion.ig_hbm, bf16[8,2048,1408]{2,1,0:T(8,128)(2,1)} %w1_hbm.1, bf16[8,2048,1408]{2,1,0:T(8,128)(2,1)} %w3_hbm.1, bf16[8,1408,2048]{2,1,0:T(8,128)(2,1)} %w2_hbm.1), custom_call_target="tpu_custom_call" | custom-call | tf_op jit(solution)/shard_map/pallas_call | solution.py:507
  215.1 2.3 %copy.8 = bf16[256,2048]{1,0:T(8,128)(2,1)} copy(bf16[256,2048]{1,0:T(8,128)(2,1)} %shard_map.64) | data formatting | bytes 2097152
  (1 shorter events, 0.0 us)

commit v3 on v2

--- a/solution.py
+++ b/solution.py
@@ -24,9 +24,9 @@
     return lax.broadcasted_iota(jnp.int32, shape, dim)
 
 
-def _kernel(cap, hot, x_hbm, ig_hbm, w1_hbm, w3_hbm, w2_hbm, out_ref,
-            xall, mall, pos, xg, xhot, u, uhot, wbuf, wtail, w2buf, s_all, s_hot, hbuf, hhot,
-            pown, psib, drecv, frecv, nrecv, cat, pmat, tri,
+def _kernel(cap, hot, x_hbm, idx_hbm, g_hbm, w1_hbm, w3_hbm, w2_hbm, out_ref,
+            xall, mall, pos, xg, xhot, u, uhot, wbuf, wtail, w2buf, s_all, hbuf,
+            pown, psib, drecv, frecv, nrecv, cat, pmat, phot, tri, idx_v, g_v, turn,
             loc_sem, xsend_s, xsend_r, xsend_l, xrecv, msend, mrecv,
             wsem, w2sem, dsend, drs, fsend, frs, nsend, nrs, credit):
     me = lax.axis_index('expert')
@@ -37,6 +37,7 @@
 
     sib, right, left, far = dev(0, 1 - k), dev(1, k), dev(3, k), dev(2, k)
     t, d = x_hbm.shape
+    top = idx_hbm.shape[1]
     el, _, ff = w1_hbm.shape
     nf = ff // FC
     tail = ff - nf * FC
@@ -46,6 +47,7 @@
     pt = t // PIECES
     hp = PIECES // 2
     rows = CHIPS * cap
+    wide = el * cap + extra
 
     def remote(src, dst, ss, rs, to):
         return pltpu.make_async_remote_copy(src_ref=src, dst_ref=dst, send_sem=ss, recv_sem=rs,
@@ -58,13 +60,16 @@
         return [pltpu.make_async_copy(w.at[e, :, pl.ds(nf * FC, tail)], wtail.at[:, pl.ds(s * tail, tail)], wsem.at[nf, s])
                 for s, w in enumerate((w1_hbm, w3_hbm))]
 
-    def w2_copy(q, e):
+    def w2_ref(odd, e):
+        return xall.at[pl.ds(0, ff), pl.ds(e * DC, DC)] if odd else w2buf.at[e]
+
+    def w2_copy(q, odd, e):
         cols = pl.ds(pl.multiple_of(q * DC, DC), DC)
-        return pltpu.make_async_copy(w2_hbm.at[e, :, cols], w2buf.at[e], w2sem.at[e])
+        return pltpu.make_async_copy(w2_hbm.at[e, :, cols], w2_ref(odd, e), w2sem.at[odd, e])
 
     def piece(b, p, ss, to):
-        r = pl.ds(p * pt, pt)
-        return remote(xall.at[b, r], xall.at[b, r], ss, xrecv.at[b, p], to)
+        r = pl.ds(pl.multiple_of(b * t + p * pt, pt), pt)
+        return remote(xall.at[r], xall.at[r], ss, xrecv.at[b, p], to)
 
     def meta(b, ss, to):
         return remote(mall.at[b], mall.at[b], ss, mrecv.at[b], to)
@@ -129,6 +134,9 @@
     def wait_block(b):
         for p in range(PIECES):
             got(b, p)
+
+    def spot(o):
+        return {0: 0, 3: 1, 1: 2, 2: 3}[o]
 
     def gather(beta, o):
         b = dev(o, beta)
@@ -145,28 +153,42 @@
         row = _iota((cap, t), 0).astype(F32)
         for e in range(el):
             pmat[e] = (rank[e:e + 1, :] == row).astype(BF16)
-        sel = pmat[...].reshape(el * cap, t)
+        hrow = _iota((extra, t), 0).astype(F32) + float(cap)
+        phot[...] = jnp.logical_and(rank[0:1, :] == hrow, me == 0).astype(BF16)
+        block = pl.ds(pl.multiple_of(b * t, t), t)
 
         def cols(j, _):
             w = pl.ds(pl.multiple_of(j * 512, 512), 512)
-            r = _dot(sel, xall[b, :, w]).astype(BF16).reshape(el, cap, 512)
+            xb = xall[block, w]
+            r = _dot(pmat[...].reshape(el * cap, t), xb).astype(BF16).reshape(el, cap, 512)
             for e in range(el):
                 xg[e, o, :, w] = r[e]
+            xhot[spot(o), :, w] = _dot(phot[...], xb).astype(BF16)
             return 0
 
-        lax.fori_loop(0, d // 512, cols, 0)
+        lax.fori_loop(0, d // 512, cols, 0, unroll=True)
+
+    def act(r, w, width):
+        ab = _dot(r, w)
+        a, b = ab[:, :width], ab[:, width:]
+        return (a * jax.nn.sigmoid(a) * b).astype(BF16)
+
+    def up_hot(blocks, f, w_ref, width):
+        lo, hi = blocks
+        uhot[lo * extra:hi * extra, f * FC:f * FC + width] = act(xhot[lo:hi].reshape((hi - lo) * extra, d), w_ref[...], width)
+
+    def w_slot(f):
+        return (wbuf.at[f], FC) if f < nf else (wtail, tail)
+
+    def up_hot_near():
+        for f in range(nf + 1):
+            for cp in w_copies(0, f):
+                cp.wait()
 
         @pl.when(me == 0)
         def _():
-            hrow = _iota((extra, t), 0).astype(F32) + float(cap)
-            hsel = (rank[0:1, :] == hrow).astype(BF16)
-
-            def hcols(j, _):
-                w = pl.ds(pl.multiple_of(j * 512, 512), 512)
-                xhot[o, :, w] = _dot(hsel, xall[b, :, w]).astype(BF16)
-                return 0
-
-            lax.fori_loop(0, d // 512, hcols, 0)
+            for f in range(nf + 1):
+                up_hot((0, CHIPS - 1), f, *w_slot(f))
 
     def up(beta, hook):
         def body(i, _):
@@ -175,27 +197,18 @@
             hook(i)
             lhs = xg[e].reshape(rows, d)
 
-            def act(r, w, width):
-                ab = _dot(r, w)
-                a, b = ab[:, :width], ab[:, width:]
-                return (a * jax.nn.sigmoid(a) * b).astype(BF16)
-
             for f in range(nf + 1):
-                if beta == 0:
+                @pl.when(i > 0)
+                def _():
                     for cp in w_copies(e, f):
                         cp.wait()
-                else:
-                    @pl.when(i > 0)
-                    def _():
-                        for cp in w_copies(e, f):
-                            cp.wait()
-                w_ref, width = (wbuf.at[f], FC) if f < nf else (wtail, tail)
+                w_ref, width = w_slot(f)
                 w_cols = pl.ds(f * FC, width)
                 u[e, :, w_cols] = act(lhs, w_ref[...], width)
 
                 @pl.when(jnp.logical_and(me == 0, e == 0))
                 def _():
-                    uhot[:, w_cols] = act(xhot[...].reshape(CHIPS * extra, d), w_ref[...], width)
+                    up_hot((CHIPS - 1 if beta == 0 else 0, CHIPS), f, w_ref, width)
 
                 @pl.when(i + 1 < el)
                 def _():
@@ -253,79 +266,64 @@
         r1 = cols - g1.astype(F32)
         g2 = r1.astype(BF16)
         g3 = (r1 - g2.astype(F32)).astype(BF16)
-        lane = _iota((1, el * cap), 1)
-        slot_e = jnp.zeros((1, el * cap), jnp.int32)
+        lane = _iota((1, wide), 1)
+        slot_e = jnp.zeros((1, wide), jnp.int32)
         for e in range(1, el):
             slot_e = slot_e + (lane >= e * cap).astype(jnp.int32)
         want = (lane - cap * slot_e).astype(F32)
         depth = cat.shape[0]
 
         def build(o, _):
-            rr = _iota((depth, el * cap), 0)
-            ll = _iota((depth, el * cap), 1)
-            lo = (rr - o * el) * cap
-            pick = jnp.logical_and(ll >= lo, ll < lo + cap).astype(BF16)
-            lo2 = lo - CHIPS * el * cap
-            pick2 = jnp.logical_and(ll >= lo2, ll < lo2 + cap).astype(BF16)
-            hit = _dot(g1, pick) == want
+            rr = _iota((depth, wide), 0)
+            ll = _iota((depth, wide), 1)
+
+            def pick(first):
+                lo = (rr - first) * cap
+                cold = jnp.logical_and(jnp.logical_and(ll >= lo, ll < lo + cap), ll < el * cap)
+                more = jnp.logical_and(jnp.logical_and(rr == first, ll >= el * cap), me == 0)
+                return jnp.logical_or(cold, more).astype(BF16)
+
+            gate = pick((CHIPS + o) * el)
+            hit = _dot(g1, pick(o * el)) == want
             for s, gs in enumerate((g1, g2, g3)):
-                s_all[o, s] = jnp.where(hit, _dot(gs, pick2), 0.0).astype(BF16)
-
-            @pl.when(me == 0)
-            def _():
-                rh = _iota((depth, extra), 0)
-                hpick = (rh == o * el).astype(BF16)
-                hpick2 = (rh == (CHIPS + o) * el).astype(BF16)
-                hhit = _dot(g1, hpick) == (_iota((t, extra), 1) + cap).astype(F32)
-                for s, gs in enumerate((g1, g2, g3)):
-                    s_hot[o, s] = jnp.where(hhit, _dot(gs, hpick2), 0.0).astype(BF16)
-
+                s_all[o, s] = jnp.where(hit, _dot(gs, gate), 0.0).astype(BF16)
             return 0
 
         lax.fori_loop(0, CHIPS, build, 0)
 
-    def chunk(beta, q):
-        def down(e, _):
-            w2_copy(q, e).wait()
-            h = _dot(u[e], w2buf[e]).astype(BF16).reshape(CHIPS, cap, DC)
+    def chunk(beta, q, odd):
+        def next_w2():
+            nxt = (q + 1) % nq
+            for e in range(el):
+                w2_copy(nxt, 1 - odd, e).start()
+
+        if beta == 0 or not odd:
+            next_w2()
+        else:
+            pl.when(q + 1 < nq)(next_w2)
+        for e0 in range(0, el, 8):
+            for e in range(e0, e0 + 8):
+                w2_copy(q, odd, e).wait()
+            for e in range(e0, e0 + 8):
+                h = _dot(u[e], w2_ref(odd, e)[...]).astype(BF16).reshape(CHIPS, cap, DC)
+                for o in range(CHIPS):
+                    hbuf[o, e * cap:(e + 1) * cap] = h[o]
+
+        @pl.when(me == 0)
+        def _():
+            h = _dot(uhot[...], w2_ref(odd, 0)[...]).astype(BF16).reshape(CHIPS, extra, DC)
             for o in range(CHIPS):
-                hbuf[o, e] = h[o]
-
-            @pl.when(jnp.logical_and(me == 0, e == 0))
-            def _():
-                hhot[...] = _dot(uhot[...], w2buf[e]).astype(BF16).reshape(CHIPS, extra, DC)
-
-            if beta == 0:
-                w2_copy((q + 1) % nq, e).start()
-            else:
-                @pl.when(q + 1 < nq)
-                def _():
-                    w2_copy(jnp.minimum(q + 1, nq - 1), e).start()
-
-            return 0
-
-        lax.fori_loop(0, el, down, 0)
+                hbuf[o, el * cap:] = h[spot(o)]
 
         @pl.when(jnp.logical_and(k != beta, q >= 2))
         def _():
             d_copy(q - 2).wait_send()
 
-        def scatter(o, _):
-            r = _dot(s_all[o].reshape(3 * t, el * cap), hbuf[o].reshape(el * cap, DC))
-            r = r[:t] + r[t:2 * t] + r[2 * t:]
+        for o in range(CHIPS):
+            hb = hbuf[o]
+            r = _dot(s_all[o, 0], hb) + _dot(s_all[o, 1], hb) + _dot(s_all[o, 2], hb)
             psib[q % 2, o, 0] = r[:, :half]
             psib[q % 2, o, 1] = r[:, half:]
-
-            @pl.when(me == 0)
-            def _():
-                z = _dot(s_hot[o].reshape(3 * t, extra), hhot[o])
-                z = z[:t] + z[t:2 * t] + z[2 * t:]
-                psib[q % 2, o, 0] = psib[q % 2, o, 0] + z[:, :half]
-                psib[q % 2, o, 1] = psib[q % 2, o, 1] + z[:, half:]
-
-            return 0
-
-        lax.fori_loop(0, CHIPS, scatter, 0)
 
         @pl.when(k != beta)
         def _():
@@ -335,60 +333,71 @@
             d_copy(q).start()
 
     def down_phase(beta):
-        build_scatter()
-        last = nq + 1 if beta == 0 else nq + 3
-
-        def step(i, _):
-            @pl.when(jnp.logical_and(k == beta, jnp.logical_and(i >= 1, i <= nq)))
-            def _():
-                pair_add(i - 1)
-
-            if beta == 0:
-                for at, q in ((3, 0), (5, 1), (7, 2)):
-                    @pl.when(jnp.logical_and(k == beta, i == at))
+        def step(j, _):
+            for odd in range(2):
+                i = 2 * j + odd
+
+                @pl.when(jnp.logical_and(k == beta, i >= 1))
+                def _():
+                    pair_add(i - 1)
+
+                if beta == 0 and odd:
+                    @pl.when(jnp.logical_and(k == beta, i >= 3))
                     def _():
-                        relay_add(q)
-            else:
-                @pl.when(jnp.logical_and(k == beta, i >= 3))
-                def _():
-                    relay_add(i - 3)
-
-            @pl.when(i < nq)
-            def _():
-                chunk(beta, i)
-
+                        relay_add(j - 1)
+                if beta == 1:
+                    @pl.when(jnp.logical_and(k == beta, i >= 3))
+                    def _():
+                        relay_add(i - 3)
+
+                chunk(beta, i, odd)
             return 0
 
-        lax.fori_loop(0, last, step, 0)
+        lax.fori_loop(0, nq // 2, step, 0)
+
+        @pl.when(k == beta)
+        def _():
+            pair_add(nq - 1)
+            if beta == 1:
+                for q in range(nq - 3, nq):
+                    relay_add(q)
 
         @pl.when(k != beta)
         def _():
             for q in range(nq - 2, nq):
                 d_copy(q).wait_send()
 
-    own = pltpu.make_async_copy(x_hbm, xall.at[me], loc_sem.at[0])
-    own_m = pltpu.make_async_copy(ig_hbm, mall.at[me], loc_sem.at[1])
+    own = pltpu.make_async_copy(x_hbm, xall.at[pl.ds(pl.multiple_of(me * t, t), t)], loc_sem.at[0])
+    own_i = pltpu.make_async_copy(idx_hbm, idx_v, loc_sem.at[1])
+    own_g = pltpu.make_async_copy(g_hbm, g_v, loc_sem.at[2])
     own.start()
-    own_m.start()
+    own_i.start()
+    own_g.start()
+    turn[...] = jnp.full(turn.shape, -1.0, F32)
     barrier = pltpu.get_barrier_semaphore()
     for peer in (sib, right, left):
         pl.semaphore_signal(barrier, inc=1, device_id={'expert': peer}, device_id_type=MESH)
     pl.semaphore_wait(barrier, 3)
     own.wait()
-    own_m.wait()
+
+    @pl.when(k == 0)
+    def _():
+        send_own()
+
+    own_i.wait()
+    own_g.wait()
+    turn[:, 0:top] = idx_v[...].astype(F32)
+    turn[:, 8:8 + top] = g_v[...]
+    mall[me] = jnp.transpose(turn[...])[0:16]
     metas = [meta(me, msend.at[0], sib), meta(me, msend.at[1], right), meta(me, msend.at[2], left)]
     for cp in metas:
         cp.start()
-
-    @pl.when(k == 0)
-    def _():
-        send_own()
-
     for f in range(nf + 1):
         for cp in w_copies(0, f):
             cp.start()
     for e in range(el):
-        w2_copy(0, e).start()
+        w2_copy(0, 0, e).start()
+    hbuf[:, el * cap:, :] = jnp.zeros((CHIPS, extra, DC), BF16)
     tri[...] = (_iota((t, t), 0) < _iota((t, t), 1)).astype(BF16)
 
     got_meta(left)
@@ -425,6 +434,7 @@
 
     gather(0, 3)
     gather(0, 1)
+    up_hot_near()
 
     @pl.when(k == 0)
     def _():
@@ -438,6 +448,8 @@
     gather(0, 2)
 
     def hook_first(i):
+        pl.when(i == 5)(build_scatter)
+
         @pl.when(k == 1)
         def _():
             for at, p in ((1, 0), (2, 1)):
@@ -456,7 +468,6 @@
                 far_in()
 
     up(0, hook_first)
-    down_phase(0)
 
     @pl.when(k == 0)
     def _():
@@ -465,8 +476,13 @@
 
     for o in range(CHIPS):
         gather(1, o)
+    for cp in token_sends():
+        cp.wait_send()
+    down_phase(0)
 
     def hook_second(i):
+        pl.when(i == 5)(build_scatter)
+
         @pl.when(jnp.logical_and(k == 0, i < nq - 3))
         def _():
             relay_add(3 + i)
@@ -476,8 +492,6 @@
     lax.fori_loop(0, nq, finish, 0)
 
     for cp in metas:
-        cp.wait_send()
-    for cp in token_sends():
         cp.wait_send()
     for q in range(nq):
         for cp in f_copies(q) + n_copies(q):
@@ -500,31 +514,31 @@
         half = DC // 2
         nf, nq = ff // FC, d // DC
         tail = ff - nf * FC
-        pad = jnp.full((8 - k, t), -1.0, F32)
-        ig = jnp.concatenate([idx.T.astype(F32), pad, g.T, pad])
+        assert k <= 8
         dma, any_ = pltpu.SemaphoreType.DMA, pl.BlockSpec(memory_space=pl.ANY)
         vm = pltpu.VMEM
         return pl.pallas_call(
             functools.partial(_kernel, cap, hot),
             out_shape=jax.ShapeDtypeStruct((t, d), BF16),
-            in_specs=[any_] * 5,
+            in_specs=[any_] * 6,
             out_specs=pl.BlockSpec(memory_space=pltpu.VMEM),
             scratch_shapes=[
-                vm((n, t, d), BF16), vm((n, 16, t), F32), vm((2, CHIPS, el, t), F32),
+                vm((n * t, d), BF16), vm((n, 16, t), F32), vm((2, CHIPS, el, t), F32),
                 vm((el, CHIPS, cap, d), BF16), vm((CHIPS, extra, d), BF16),
                 vm((el, CHIPS * cap, ff), BF16), vm((CHIPS * extra, ff), BF16),
                 vm((nf, d, 2 * FC), BF16), vm((d, 2 * tail), BF16), vm((el, ff, DC), BF16),
-                vm((CHIPS, 3, t, el * cap), BF16), vm((CHIPS, 3, t, extra), BF16),
-                vm((CHIPS, el, cap, DC), BF16), vm((CHIPS, extra, DC), BF16),
+                vm((CHIPS, 3, t, el * cap + extra), BF16),
+                vm((CHIPS, el * cap + extra, DC), BF16),
                 vm((nq, CHIPS, 2, t, half), F32), vm((2, CHIPS, 2, t, half), F32), vm((2, CHIPS, 2, t, half), F32),
                 vm((nq, 2, t, half), F32), vm((nq, 2, 2, t, half), F32),
-                vm((-(-2 * CHIPS * el // 128) * 128, t), F32), vm((el, cap, t), BF16), vm((t, t), BF16),
-                dma((2,)), dma((CHIPS, PIECES)), dma((2 * PIECES,)), dma((2 * PIECES,)), dma((n, PIECES)), dma((7,)), dma((n,)),
-                dma((nf + 1, 2)), dma((el,)), dma((2,)), dma((2,)), dma((nq, 2)), dma((nq, 2)), dma((nq, 2)), dma((nq, 2)),
+                vm((-(-2 * CHIPS * el // 128) * 128, t), F32), vm((el, cap, t), BF16), vm((extra, t), BF16), vm((t, t), BF16),
+                vm((t, k), jnp.int32), vm((t, k), F32), vm((t, 128), F32),
+                dma((3,)), dma((CHIPS, PIECES)), dma((2 * PIECES,)), dma((2 * PIECES,)), dma((n, PIECES)), dma((7,)), dma((n,)),
+                dma((nf + 1, 2)), dma((2, el)), dma((2,)), dma((2,)), dma((nq, 2)), dma((nq, 2)), dma((nq, 2)), dma((nq, 2)),
                 pltpu.SemaphoreType.REGULAR,
             ],
             compiler_params=pltpu.CompilerParams(collective_id=0, has_side_effects=True, vmem_limit_bytes=67043328),
-        )(x, ig, w1, w3, w2)
+        )(x, idx, g, w1, w3, w2)
 
     rows = P(('data', 'expert'))
     wspec = P('expert')

time: 218 us -> 178 us (0.82)
  Pallas kernels: 213 us -> 173 us
  local copies, waits for them, and re-layouts: 2.31 us -> 5.28 us
    pallas_call x1, Pallas kernels: 213 us -> 173 us  [local(): pl.pallas_call(functools.partial(_kernel, cap, hot), out_shape=jax.ShapeD...]
    unnamed x1 -> x3, local copies, waits for them, and re-layouts: 2.3 us -> 5.28 us
where the time goes in v3:
time: 178 us
  Pallas kernels  173 us (97%)
  local copies, waits for them, and re-layouts  5.28 us (3%)
    pallas_call x1, Pallas kernels, local(): pl.pallas_call(functools.partial(_kernel, cap, hot), out_shape=jax.ShapeD...  173 us
    unnamed x3, local copies, waits for them, and re-layouts  5.28 us

profile of v3, /device:TPU:113, one launch (start us, length us, event | category | flops | bytes accessed | tf_op | source)
XLA Modules:
  0.0 178.0 jit_solution(1985764210587570060)
XLA Ops:
  0.0 1.5 copy.7.idx_hbm
  1.5 1.5 copy.8.g_hbm
  3.0 172.7 %shard_map.64 = bf16[256,2048]{1,0:T(8,128)(2,1)} custom-call(bf16[256,2048]{1,0:T(8,128)(2,1)} %x_hbm.1, s32[256,6]{1,0:T(8,128)} %copy.7.idx_hbm, f32[256,6]{1,0:T(8,128)} %copy.8.g_hbm, bf16[8,2048,1408]{2,1,0:T(8,128)(2,1)} %w1_hbm.1, bf16[8,2048,1408]{2,1,0:T(8,128)(2,1)} %w3_hbm.1, bf16[8,1408,2048]{2,1,0:T(8,128)(2,1)} %w2_hbm.1), custom_call_target="tpu_custom_call" | custom-call | tf_op jit(solution)/shard_map/pallas_call | solution.py:520
  175.7 2.3 %copy.10 = bf16[256,2048]{1,0:T(8,128)(2,1)} copy(bf16[256,2048]{1,0:T(8,128)(2,1)} %shard_map.64) | data formatting | bytes 2097152

commit v4 on v3

--- a/solution.py
+++ b/solution.py
@@ -26,7 +26,7 @@
 
 def _kernel(cap, hot, x_hbm, idx_hbm, g_hbm, w1_hbm, w3_hbm, w2_hbm, out_ref,
             xall, mall, pos, xg, xhot, u, uhot, wbuf, wtail, w2buf, s_all, hbuf,
-            pown, psib, drecv, frecv, nrecv, cat, pmat, phot, tri, idx_v, g_v, turn,
+            pown, psib, drecv, frecv, nrecv, cat, pmat, phot, tri, idx_v, g_v, routes,
             loc_sem, xsend_s, xsend_r, xsend_l, xrecv, msend, mrecv,
             wsem, w2sem, dsend, drs, fsend, frs, nsend, nrs, credit):
     me = lax.axis_index('expert')
@@ -37,7 +37,7 @@
 
     sib, right, left, far = dev(0, 1 - k), dev(1, k), dev(3, k), dev(2, k)
     t, d = x_hbm.shape
-    top = idx_hbm.shape[1]
+    top = idx_hbm.shape[0]
     el, _, ff = w1_hbm.shape
     nf = ff // FC
     tail = ff - nf * FC
@@ -139,7 +139,8 @@
         return {0: 0, 3: 1, 1: 2, 2: 3}[o]
 
     def gather(beta, o):
-        b = dev(o, beta)
+        b = dev(o, 1 - beta)
+        pl.when(b != me)(lambda: got_meta(b))
         ids = mall[b, 0:8]
         gts = mall[b, 8:16]
         for e in range(el):
@@ -315,7 +316,7 @@
             for o in range(CHIPS):
                 hbuf[o, el * cap:] = h[spot(o)]
 
-        @pl.when(jnp.logical_and(k != beta, q >= 2))
+        @pl.when(jnp.logical_and(k == beta, q >= 2))
         def _():
             d_copy(q - 2).wait_send()
 
@@ -325,7 +326,7 @@
             psib[q % 2, o, 0] = r[:, :half]
             psib[q % 2, o, 1] = r[:, half:]
 
-        @pl.when(k != beta)
+        @pl.when(k == beta)
         def _():
             @pl.when(q >= 2)
             def _():
@@ -337,16 +338,16 @@
             for odd in range(2):
                 i = 2 * j + odd
 
-                @pl.when(jnp.logical_and(k == beta, i >= 1))
+                @pl.when(jnp.logical_and(k != beta, i >= 1))
                 def _():
                     pair_add(i - 1)
 
                 if beta == 0 and odd:
-                    @pl.when(jnp.logical_and(k == beta, i >= 3))
+                    @pl.when(jnp.logical_and(k != beta, i >= 3))
                     def _():
                         relay_add(j - 1)
                 if beta == 1:
-                    @pl.when(jnp.logical_and(k == beta, i >= 3))
+                    @pl.when(jnp.logical_and(k != beta, i >= 3))
                     def _():
                         relay_add(i - 3)
 
@@ -355,14 +356,14 @@
 
         lax.fori_loop(0, nq // 2, step, 0)
 
-        @pl.when(k == beta)
+        @pl.when(k != beta)
         def _():
             pair_add(nq - 1)
             if beta == 1:
                 for q in range(nq - 3, nq):
                     relay_add(q)
 
-        @pl.when(k != beta)
+        @pl.when(k == beta)
         def _():
             for q in range(nq - 2, nq):
                 d_copy(q).wait_send()
@@ -373,25 +374,26 @@
     own.start()
     own_i.start()
     own_g.start()
-    turn[...] = jnp.full(turn.shape, -1.0, F32)
     barrier = pltpu.get_barrier_semaphore()
-    for peer in (sib, right, left):
+    peers = [far, right, left, sib] + [dev(o, 1 - k) for o in (2, 1, 3)]
+    for peer in peers:
         pl.semaphore_signal(barrier, inc=1, device_id={'expert': peer}, device_id_type=MESH)
-    pl.semaphore_wait(barrier, 3)
+    pl.semaphore_wait(barrier, len(peers))
     own.wait()
-
-    @pl.when(k == 0)
-    def _():
-        send_own()
-
     own_i.wait()
     own_g.wait()
-    turn[:, 0:top] = idx_v[...].astype(F32)
-    turn[:, 8:8 + top] = g_v[...]
-    mall[me] = jnp.transpose(turn[...])[0:16]
-    metas = [meta(me, msend.at[0], sib), meta(me, msend.at[1], right), meta(me, msend.at[2], left)]
+    routes[...] = jnp.full(routes.shape, -1.0, F32)
+    routes[0:top] = idx_v[...].astype(F32)
+    routes[8:8 + top] = g_v[...]
+    mall[me] = routes[...]
+    metas = [meta(me, msend.at[j], to) for j, to in enumerate(peers)]
     for cp in metas:
         cp.start()
+
+    @pl.when(k == 1)
+    def _():
+        send_own()
+
     for f in range(nf + 1):
         for cp in w_copies(0, f):
             cp.start()
@@ -400,26 +402,13 @@
     hbuf[:, el * cap:, :] = jnp.zeros((CHIPS, extra, DC), BF16)
     tri[...] = (_iota((t, t), 0) < _iota((t, t), 1)).astype(BF16)
 
-    got_meta(left)
-    metas += [meta(left, msend.at[3], right), meta(left, msend.at[4], sib)]
-    metas[3].start()
-    metas[4].start()
-    got_meta(right)
-    metas += [meta(right, msend.at[5], sib)]
-    metas[5].start()
-    got_meta(far)
-    metas += [meta(far, msend.at[6], sib)]
-    metas[6].start()
-    for o in range(CHIPS):
-        got_meta(dev(o, 1 - k))
+    @pl.when(k == 0)
+    def _():
+        wait_block(dev(0, 1))
+
+    gather(0, 0)
 
     @pl.when(k == 1)
-    def _():
-        wait_block(dev(0, 0))
-
-    gather(0, 0)
-
-    @pl.when(k == 0)
     def _():
         for p in range(hp):
             relay(p)
@@ -427,22 +416,22 @@
         rest_near()
         sib_near(False)
 
-    @pl.when(k == 1)
-    def _():
-        wait_block(dev(3, 0))
-        wait_block(dev(1, 0))
+    @pl.when(k == 0)
+    def _():
+        wait_block(dev(3, 1))
+        wait_block(dev(1, 1))
 
     gather(0, 3)
     gather(0, 1)
     up_hot_near()
 
+    @pl.when(k == 1)
+    def _():
+        far_in()
+
     @pl.when(k == 0)
     def _():
-        far_in()
-
-    @pl.when(k == 1)
-    def _():
-        wait_block(dev(2, 0))
+        wait_block(dev(2, 1))
         send_own()
 
     gather(0, 2)
@@ -450,7 +439,7 @@
     def hook_first(i):
         pl.when(i == 5)(build_scatter)
 
-        @pl.when(k == 1)
+        @pl.when(k == 0)
         def _():
             for at, p in ((1, 0), (2, 1)):
                 @pl.when(i == at)
@@ -469,10 +458,10 @@
 
     up(0, hook_first)
 
-    @pl.when(k == 0)
+    @pl.when(k == 1)
     def _():
         for o in range(CHIPS):
-            wait_block(dev(o, 1))
+            wait_block(dev(o, 0))
 
     for o in range(CHIPS):
         gather(1, o)
@@ -483,7 +472,7 @@
     def hook_second(i):
         pl.when(i == 5)(build_scatter)
 
-        @pl.when(jnp.logical_and(k == 0, i < nq - 3))
+        @pl.when(jnp.logical_and(k == 1, i < nq - 3))
         def _():
             relay_add(3 + i)
 
@@ -532,13 +521,13 @@
                 vm((nq, CHIPS, 2, t, half), F32), vm((2, CHIPS, 2, t, half), F32), vm((2, CHIPS, 2, t, half), F32),
                 vm((nq, 2, t, half), F32), vm((nq, 2, 2, t, half), F32),
                 vm((-(-2 * CHIPS * el // 128) * 128, t), F32), vm((el, cap, t), BF16), vm((extra, t), BF16), vm((t, t), BF16),
-                vm((t, k), jnp.int32), vm((t, k), F32), vm((t, 128), F32),
+                vm((k, t), jnp.int32), vm((k, t), F32), vm((16, t), F32),
                 dma((3,)), dma((CHIPS, PIECES)), dma((2 * PIECES,)), dma((2 * PIECES,)), dma((n, PIECES)), dma((7,)), dma((n,)),
                 dma((nf + 1, 2)), dma((2, el)), dma((2,)), dma((2,)), dma((nq, 2)), dma((nq, 2)), dma((nq, 2)), dma((nq, 2)),
                 pltpu.SemaphoreType.REGULAR,
             ],
             compiler_params=pltpu.CompilerParams(collective_id=0, has_side_effects=True, vmem_limit_bytes=67043328),
-        )(x, idx, g, w1, w3, w2)
+        )(x, idx.T, g.T, w1, w3, w2)
 
     rows = P(('data', 'expert'))
     wspec = P('expert')

time: 178 us -> 168 us (0.944)
  the two profiles are of different devices: /device:TPU:113 before, /device:TPU:112 now
where the time goes in v4:
time: 168 us
  Pallas kernels  165 us (98%)
  local copies, waits for them, and re-layouts  2.3 us (1%)
    pallas_call x1, Pallas kernels, local(): pl.pallas_call(functools.partial(_kernel, cap, hot), out_shape=jax.ShapeD...  165 us

profile of v4, /device:TPU:112, one launch (start us, length us, event | category | flops | bytes accessed | tf_op | source)
XLA Modules:
  0.0 167.6 jit_solution(7076403687258156426)
XLA Ops:
  0.0 165.3 %shard_map.64 = bf16[256,2048]{1,0:T(8,128)(2,1)} custom-call(bf16[256,2048]{1,0:T(8,128)(2,1)} %x_hbm.1, s32[6,256]{1,0:T(8,128)} %bitcast.2, f32[6,256]{1,0:T(8,128)} %bitcast.3, bf16[8,2048,1408]{2,1,0:T(8,128)(2,1)} %w1_hbm.1, bf16[8,2048,1408]{2,1,0:T(8,128)(2,1)} %w3_hbm.1, bf16[8,1408,2048]{2,1,0:T(8,128)(2,1)} %w2_hbm.1), custom_call_target="tpu_custom_call" | custom-call | tf_op jit(solution)/shard_map/pallas_call | solution.py:509
  165.3 2.3 %copy.8 = bf16[256,2048]{1,0:T(8,128)(2,1)} copy(bf16[256,2048]{1,0:T(8,128)(2,1)} %shard_map.64) | data formatting | bytes 2097152
